TPU v7x, 32 devices: a whole 2x2x4 slice. The times are simulated.
32 devices in a mesh: cp: 16 (over z, x, core), tp: 2 (over y).
Axes of the slice: x: 2, y: 2, z: 4, core: 2. Of those that a mesh axis runs over, the one named last changes fastest.
Arguments:
- query: bfloat16 [1024, 16384], P(('cp', 'tp')), may hold values from -6 to 6
- fresh_key_rows: bfloat16 [1024, 1024], P(('cp', 'tp')), may hold values from -6 to 6
- fresh_value_rows: bfloat16 [1024, 1024], P(('cp', 'tp')), may hold values from -6 to 6
- cached_key_rows: bfloat16 [8192, 1024], P('cp', 'tp'), may hold values from -6 to 6
- cached_value_rows: bfloat16 [8192, 1024], P('cp', 'tp'), may hold values from -6 to 6
- prefix_len: int32 [1], replicated, may hold values from 4096 to 8192
- stripe_owner: int32 [16], replicated, may hold values from 0 to 15, each once
Outputs:
- attended: bfloat16 [1024, 16384], P('cp', 'tp')
Inputs may be any that keep to these rules, and one draw needn't show every extreme that they name: `stripe_owner`: a permutation of 0 to 15.
All inputs are finite; a program needn't handle non-finite values.
Results may differ from a plain program's by a relative error of at most 0.0075.
Values may be sent and summed in bfloat16 or wider, within the bound.
A program may use at most 64 MiB of HBM per device.

v0:
```python
import jax
import jax.numpy as jnp
from jax import lax
from jax.sharding import PartitionSpec as P

HEAD_SIZE = 128


NEG = -1e30


def for_sending(array):

    def short(part):
        return part.astype(jnp.bfloat16) if part.dtype == jnp.float32 else part

    return jax.tree.map(short, array)


def shifted(value, axis, steps):
    count = lax.axis_size(axis)
    pairs = [(source, (source + steps) % count) for source in range(count)]
    return lax.ppermute(value, axis, pairs)


def natural_index(residue, rows, parts):
    stripe = rows // parts
    local = jnp.arange(rows, dtype=jnp.int32)
    return local // stripe * rows + residue * stripe + local % stripe


def attend_piece(state, queries, keys, values, visible):
    peak, total, summed = state
    heads, group_size, rows = peak.shape
    scores = jnp.einsum(
        "hqd,hkd->hqk", queries, keys, preferred_element_type=jnp.float32
    ) * HEAD_SIZE ** (-0.5)
    scores = scores.reshape(heads, group_size, rows, keys.shape[1])
    newpeak = jnp.maximum(peak, jnp.max(jnp.where(visible, scores, NEG), axis=-1))
    weights = jnp.where(visible, jnp.exp(scores - newpeak[..., None]), 0.0)
    factor = jnp.exp(peak - newpeak)
    total = factor * total + jnp.sum(weights, axis=-1)
    rounded = weights.astype(jnp.bfloat16).reshape(heads, group_size * rows, keys.shape[1])
    product = jnp.einsum("hqk,hkd->hqd", rounded, values, preferred_element_type=jnp.float32)
    summed = factor[..., None] * summed + product.reshape(heads, group_size, rows, values.shape[2])
    return (newpeak, total, summed)


def attend_block(
    state,
    queries,
    query_index,
    new_keys,
    new_values,
    key_index,
    cache_keys,
    cache_values,
    cache_start,
    plen,
):
    visible = key_index[None, :] <= query_index[:, None]
    state = attend_piece(state, queries, new_keys, new_values, visible)
    slots = cache_start + jnp.arange(cache_keys.shape[1], dtype=jnp.int32)
    live = jnp.broadcast_to((slots < plen)[None, :], (query_index.shape[0], slots.shape[0]))
    return attend_piece(state, queries, cache_keys, cache_values, live)


def shards(
    query,
    fresh_key_rows,
    fresh_value_rows,
    cached_key_rows,
    cached_value_rows,
    prefix_len,
    stripe_owner,
):
    parts = lax.axis_size("cp")
    me = lax.axis_index("cp")
    q_local, k_local, v_local = (
        lax.all_to_all(query, "tp", split_axis=1, concat_axis=0, tiled=True),
        lax.all_to_all(fresh_key_rows, "tp", split_axis=1, concat_axis=0, tiled=True),
        lax.all_to_all(fresh_value_rows, "tp", split_axis=1, concat_axis=0, tiled=True),
    )
    rows = q_local.shape[0]
    stripe = rows // parts
    order = jnp.arange(parts, dtype=jnp.int32)
    inverse = jnp.sum(jnp.where(stripe_owner[None, :] == order[:, None], order[None, :], 0), axis=1)

    def arrange(array):
        return jnp.take(array.reshape(parts, stripe, array.shape[1]), inverse, axis=0).reshape(
            rows, array.shape[1]
        )

    q_bal, k_bal, v_bal = (
        lax.all_to_all(arrange(q_local), "cp", split_axis=0, concat_axis=0, tiled=True),
        lax.all_to_all(arrange(k_local), "cp", split_axis=0, concat_axis=0, tiled=True),
        lax.all_to_all(arrange(v_local), "cp", split_axis=0, concat_axis=0, tiled=True),
    )
    heads = k_bal.shape[1] // HEAD_SIZE
    group_size = q_bal.shape[1] // HEAD_SIZE // heads
    queries = (
        q_bal.reshape(rows, heads, group_size, HEAD_SIZE)
        .transpose(1, 2, 0, 3)
        .reshape(heads, group_size * rows, HEAD_SIZE)
    )

    def by_head(array):
        return array.reshape(array.shape[0], heads, HEAD_SIZE).transpose(1, 0, 2)

    new_keys = by_head(k_bal)
    new_values = by_head(v_bal)
    cache_keys = by_head(cached_key_rows)
    cache_values = by_head(cached_value_rows)
    cache_rows = cached_key_rows.shape[0]
    plen = prefix_len[0]
    own_index = natural_index(inverse[me], rows, parts)
    empty = (
        jnp.full((heads, group_size, rows), NEG, jnp.float32),
        jnp.zeros((heads, group_size, rows), jnp.float32),
        jnp.zeros((heads, group_size, rows, HEAD_SIZE), jnp.float32),
    )
    own_block = (new_keys, new_values, cache_keys, cache_values)

    def visit_keys(state, block_number, source):
        key_index = natural_index(inverse[source], rows, parts)
        return attend_block(
            state,
            queries,
            own_index,
            block_number[0],
            block_number[1],
            key_index,
            block_number[2],
            block_number[3],
            source * cache_rows,
            plen,
        )

    state = visit_keys(empty, own_block, me)

    def step_one(turn, carry):
        current, block_number = carry
        block_number = jax.tree.map(
            lambda part, own: part.astype(own.dtype),
            shifted(for_sending(block_number), "cp", 1),
            block_number,
        )
        return (visit_keys(current, block_number, (me - turn) % parts), block_number)

    state, _ = lax.fori_loop(1, parts, step_one, (state, own_block))
    _, total, summed = state
    result = (summed / total[..., None]).astype(jnp.bfloat16)
    return result.transpose(2, 0, 1, 3).reshape(rows, heads * group_size * HEAD_SIZE)


def solution(mesh):
    return jax.shard_map(
        shards,
        mesh=mesh,
        in_specs=(
            P(("cp", "tp"), None),
            P(("cp", "tp"), None),
            P(("cp", "tp"), None),
            P("cp", "tp"),
            P("cp", "tp"),
            P(),
            P(),
        ),
        out_specs=P("cp", "tp"),
        check_vma=False,
    )
```

profile of v0, /device:TPU:0, one launch (start us, length us, event | category | flops | bytes accessed | tf_op | source)
XLA Modules:
  0.0 689.2 jit_solution(15471065119544823545)
XLA Ops:
  23.0 9.8 %all-to-all-done = bf16[32,2,8192]{2,0,1:T(8,128)(2,1)S(1)} async-done(((bf16[32,2,8192]{2,0,1:T(8,128)(2,1)}), bf16[32,2,8192]{2,0,1:T(8,128)(2,1)S(1)}, u32[]{:S(2)}, u32[]{:S(2)}) %all-to-all-start) | async-done | bytes 1048608 | tf_op jit(solution)/shard_map/all_to_all | solution.py:80
  32.8 6.1 all-to-all-start.3
  40.8 5.0 all-to-all-done.3
  50.8 5.4 all-to-all-done.5
  67.1 15.5 %all-to-all-done.1 = bf16[16,4,8192]{2,1,0:T(4,128)(2,1)S(1)} async-done(((bf16[16,4,8192]{2,1,0:T(4,128)(2,1)}), bf16[16,4,8192]{2,1,0:T(4,128)(2,1)S(1)}, u32[]{:S(2)}, u32[]{:S(2)}) %all-to-all-start.1) | async-done | bytes 1048608 | tf_op jit(solution)/shard_map/all_to_all | solution.py:95
  84.5 4.9 select_reduce_fusion.2
  105.7 579.2 %while.29 = (s32[]{:T(128)}, f32[4,16,64]{2,1,0:T(8,128)S(1)}, f32[4,16,64]{2,1,0:T(8,128)S(1)}, f32[4,16,64,128]{3,2,1,0:T(8,128)}, bf16[4,64,128]{2,1,0:T(8,12...) while((s32[]{:T(128)}, f32[4,16,64]{2,1,0:T(8,128)S(1)}, ...), condition=%wide.region_10.12_spmd.clone, body=%wide.region_5.11_spmd.clone.sunk | while | flops 1235508096 | bytes 69316208 | solution.py:150
  112.7 6.1 collective-permute-done.1
  120.1 5.1 collective-permute-done.3
  136.1 5.8 fusion.80
  149.5 7.9 %collective-permute-done.1 = bf16[4,64,128]{2,1,0:T(8,128)(2,1)S(1)} collective-permute-done((bf16[4,64,128]{2,1,0:T(8,128)(2,1)S(1)}, bf16[4,64,128]{2,1,0:T(8,128)(2,1)S(1)}, u32[]{:S(2)}, u32[]{:S(2)}) %collective-permute-start.1) | collective-permute-done | bytes 65568 | tf_op jit(solution)/shard_map/while/body/eval_jaxpr/ppermute | solution.py:23
  158.6 5.1 collective-permute-done.3
  164.3 4.6 select_reduce_fusion.7
  174.6 5.8 fusion.80
  186.2 9.7 %collective-permute-done.1 = bf16[4,64,128]{2,1,0:T(8,128)(2,1)S(1)} collective-permute-done((bf16[4,64,128]{2,1,0:T(8,128)(2,1)S(1)}, bf16[4,64,128]{2,1,0:T(8,128)(2,1)S(1)}, u32[]{:S(2)}, u32[]{:S(2)}) %collective-permute-start.1) | collective-permute-done | bytes 65568 | tf_op jit(solution)/shard_map/while/body/eval_jaxpr/ppermute | solution.py:23
  197.2 5.1 collective-permute-done.3
  202.9 4.6 select_reduce_fusion.7
  213.2 5.8 fusion.80
  224.8 9.7 %collective-permute-done.1 = bf16[4,64,128]{2,1,0:T(8,128)(2,1)S(1)} collective-permute-done((bf16[4,64,128]{2,1,0:T(8,128)(2,1)S(1)}, bf16[4,64,128]{2,1,0:T(8,128)(2,1)S(1)}, u32[]{:S(2)}, u32[]{:S(2)}) %collective-permute-start.1) | collective-permute-done | bytes 65568 | tf_op jit(solution)/shard_map/while/body/eval_jaxpr/ppermute | solution.py:23
  235.7 5.1 collective-permute-done.3
  241.4 4.6 select_reduce_fusion.7
  251.7 5.8 fusion.80
  263.3 9.7 %collective-permute-done.1 = bf16[4,64,128]{2,1,0:T(8,128)(2,1)S(1)} collective-permute-done((bf16[4,64,128]{2,1,0:T(8,128)(2,1)S(1)}, bf16[4,64,128]{2,1,0:T(8,128)(2,1)S(1)}, u32[]{:S(2)}, u32[]{:S(2)}) %collective-permute-start.1) | collective-permute-done | bytes 65568 | tf_op jit(solution)/shard_map/while/body/eval_jaxpr/ppermute | solution.py:23
  274.3 5.1 collective-permute-done.3
  280.0 4.6 select_reduce_fusion.7
  290.3 5.8 fusion.80
  301.9 9.7 %collective-permute-done.1 = bf16[4,64,128]{2,1,0:T(8,128)(2,1)S(1)} collective-permute-done((bf16[4,64,128]{2,1,0:T(8,128)(2,1)S(1)}, bf16[4,64,128]{2,1,0:T(8,128)(2,1)S(1)}, u32[]{:S(2)}, u32[]{:S(2)}) %collective-permute-start.1) | collective-permute-done | bytes 65568 | tf_op jit(solution)/shard_map/while/body/eval_jaxpr/ppermute | solution.py:23
  312.8 5.1 collective-permute-done.3
  318.5 4.6 select_reduce_fusion.7
  328.8 5.8 fusion.80
  340.4 9.7 %collective-permute-done.1 = bf16[4,64,128]{2,1,0:T(8,128)(2,1)S(1)} collective-permute-done((bf16[4,64,128]{2,1,0:T(8,128)(2,1)S(1)}, bf16[4,64,128]{2,1,0:T(8,128)(2,1)S(1)}, u32[]{:S(2)}, u32[]{:S(2)}) %collective-permute-start.1) | collective-permute-done | bytes 65568 | tf_op jit(solution)/shard_map/while/body/eval_jaxpr/ppermute | solution.py:23
  351.4 5.1 collective-permute-done.3
  357.1 4.6 select_reduce_fusion.7
  367.4 5.8 fusion.80
  379.0 9.7 %collective-permute-done.1 = bf16[4,64,128]{2,1,0:T(8,128)(2,1)S(1)} collective-permute-done((bf16[4,64,128]{2,1,0:T(8,128)(2,1)S(1)}, bf16[4,64,128]{2,1,0:T(8,128)(2,1)S(1)}, u32[]{:S(2)}, u32[]{:S(2)}) %collective-permute-start.1) | collective-permute-done | bytes 65568 | tf_op jit(solution)/shard_map/while/body/eval_jaxpr/ppermute | solution.py:23
  389.9 5.1 collective-permute-done.3
  395.6 4.6 select_reduce_fusion.7
  405.9 5.8 fusion.80
  417.5 9.7 %collective-permute-done.1 = bf16[4,64,128]{2,1,0:T(8,128)(2,1)S(1)} collective-permute-done((bf16[4,64,128]{2,1,0:T(8,128)(2,1)S(1)}, bf16[4,64,128]{2,1,0:T(8,128)(2,1)S(1)}, u32[]{:S(2)}, u32[]{:S(2)}) %collective-permute-start.1) | collective-permute-done | bytes 65568 | tf_op jit(solution)/shard_map/while/body/eval_jaxpr/ppermute | solution.py:23
  428.5 5.1 collective-permute-done.3
  434.2 4.6 select_reduce_fusion.7
  444.5 5.8 fusion.80
  456.1 9.7 %collective-permute-done.1 = bf16[4,64,128]{2,1,0:T(8,128)(2,1)S(1)} collective-permute-done((bf16[4,64,128]{2,1,0:T(8,128)(2,1)S(1)}, bf16[4,64,128]{2,1,0:T(8,128)(2,1)S(1)}, u32[]{:S(2)}, u32[]{:S(2)}) %collective-permute-start.1) | collective-permute-done | bytes 65568 | tf_op jit(solution)/shard_map/while/body/eval_jaxpr/ppermute | solution.py:23
  467.0 5.1 collective-permute-done.3
  483.0 5.8 fusion.80
  494.6 9.7 %collective-permute-done.1 = bf16[4,64,128]{2,1,0:T(8,128)(2,1)S(1)} collective-permute-done((bf16[4,64,128]{2,1,0:T(8,128)(2,1)S(1)}, bf16[4,64,128]{2,1,0:T(8,128)(2,1)S(1)}, u32[]{:S(2)}, u32[]{:S(2)}) %collective-permute-start.1) | collective-permute-done | bytes 65568 | tf_op jit(solution)/shard_map/while/body/eval_jaxpr/ppermute | solution.py:23
  505.6 5.1 collective-permute-done.3
  521.6 5.8 fusion.80
  533.2 9.7 %collective-permute-done.1 = bf16[4,64,128]{2,1,0:T(8,128)(2,1)S(1)} collective-permute-done((bf16[4,64,128]{2,1,0:T(8,128)(2,1)S(1)}, bf16[4,64,128]{2,1,0:T(8,128)(2,1)S(1)}, u32[]{:S(2)}, u32[]{:S(2)}) %collective-permute-start.1) | collective-permute-done | bytes 65568 | tf_op jit(solution)/shard_map/while/body/eval_jaxpr/ppermute | solution.py:23
  544.1 5.1 collective-permute-done.3
  549.8 4.6 select_reduce_fusion.7
  560.1 5.8 fusion.80
  571.7 9.7 %collective-permute-done.1 = bf16[4,64,128]{2,1,0:T(8,128)(2,1)S(1)} collective-permute-done((bf16[4,64,128]{2,1,0:T(8,128)(2,1)S(1)}, bf16[4,64,128]{2,1,0:T(8,128)(2,1)S(1)}, u32[]{:S(2)}, u32[]{:S(2)}) %collective-permute-start.1) | collective-permute-done | bytes 65568 | tf_op jit(solution)/shard_map/while/body/eval_jaxpr/ppermute | solution.py:23
  582.7 5.1 collective-permute-done.3
  588.4 4.6 select_reduce_fusion.7
  598.7 5.8 fusion.80
  610.3 9.7 %collective-permute-done.1 = bf16[4,64,128]{2,1,0:T(8,128)(2,1)S(1)} collective-permute-done((bf16[4,64,128]{2,1,0:T(8,128)(2,1)S(1)}, bf16[4,64,128]{2,1,0:T(8,128)(2,1)S(1)}, u32[]{:S(2)}, u32[]{:S(2)}) %collective-permute-start.1) | collective-permute-done | bytes 65568 | tf_op jit(solution)/shard_map/while/body/eval_jaxpr/ppermute | solution.py:23
  621.2 5.1 collective-permute-done.3
  626.9 4.6 select_reduce_fusion.7
  637.2 5.8 fusion.80
  648.8 9.7 %collective-permute-done.1 = bf16[4,64,128]{2,1,0:T(8,128)(2,1)S(1)} collective-permute-done((bf16[4,64,128]{2,1,0:T(8,128)(2,1)S(1)}, bf16[4,64,128]{2,1,0:T(8,128)(2,1)S(1)}, u32[]{:S(2)}, u32[]{:S(2)}) %collective-permute-start.1) | collective-permute-done | bytes 65568 | tf_op jit(solution)/shard_map/while/body/eval_jaxpr/ppermute | solution.py:23
  659.8 5.1 collective-permute-done.3
  665.5 4.6 select_reduce_fusion.7
  675.8 5.8 fusion.80
  (619 shorter events, 270.1 us)
Async XLA Ops:
  17.3 15.4 %all-to-all-start = ((bf16[32,2,8192]{2,0,1:T(8,128)(2,1)}), bf16[32,2,8192]{2,0,1:T(8,128)(2,1)S(1)}, u32[]{:S(2)}, u32[]{:S(2)}) async-start(bf16[32,2,8192]{2,0,1:T(8,128)(2,1)} %bitcast.60), calls=%async_computation | async-start | bytes 2097152 | tf_op jit(solution)/shard_map/all_to_all | solution.py:80
  32.8 13.0 %all-to-all-start.3 = ((bf16[16,4,512]{2,1,0:T(4,128)(2,1)}), bf16[16,4,512]{2,1,0:T(4,128)(2,1)S(1)}, u32[]{:S(2)}, u32[]{:S(2)}) async-start(bf16[16,4,512]{2,1,0:T(4,128)(2,1)} %get-tuple-element.458), calls=%async_computation.3 | async-start | bytes 131072 | tf_op jit(solution)/shard_map/all_to_all | solution.py:96
  45.8 10.4 %all-to-all-start.5 = ((bf16[16,4,512]{2,1,0:T(4,128)(2,1)}), bf16[16,4,512]{2,1,0:T(4,128)(2,1)S(1)}, u32[]{:S(2)}, u32[]{:S(2)}) async-start(bf16[16,4,512]{2,1,0:T(4,128)(2,1)} %get-tuple-element.457), calls=%async_computation.5 | async-start | bytes 131072 | tf_op jit(solution)/shard_map/all_to_all | solution.py:97
  56.2 26.5 %all-to-all-start.1 = ((bf16[16,4,8192]{2,1,0:T(4,128)(2,1)}), bf16[16,4,8192]{2,1,0:T(4,128)(2,1)S(1)}, u32[]{:S(2)}, u32[]{:S(2)}) async-start(bf16[16,4,8192]{2,1,0:T(4,128)(2,1)} %broadcast_select_fusion), calls=%async_computation.1 | async-start | bytes 2097152 | tf_op jit(solution)/shard_map/all_to_all | solution.py:95
  105.7 20.1 %collective-permute-start = (bf16[4,512,128]{2,1,0:T(8,128)(2,1)}, bf16[4,512,128]{2,1,0:T(8,128)(2,1)S(1)}, u32[]{:S(2)}, u32[]{:S(2)}) collective-permute-start(bf16[4,512,128]{2,1,0:T(8,128)(2,1)} %get-tuple-element.585), channel_id=1, source_target_pairs={{0,2},{2,4},{4,6},{6,8},{8,10},{10,12},{12,14},{14,16},{16,18},{18... | collective-permute-start | bytes 1572872 | tf_op jit(solution)/shard_map/while/body/eval_jaxpr/ppermute | solution.py:23
  106.4 12.5 %collective-permute-start.1 = (bf16[4,64,128]{2,1,0:T(8,128)(2,1)S(1)}, bf16[4,64,128]{2,1,0:T(8,128)(2,1)S(1)}, u32[]{:S(2)}, u32[]{:S(2)}) collective-permute-start(bf16[4,64,128]{2,1,0:T(8,128)(2,1)S(1)} %get-tuple-element.583), channel_id=1, source_target_pairs={{0,2},{2,4},{4,6},{6,8},{8,10},{10,12},{12,14},{14,16},{16,18},{18... | collective-permute-start | bytes 196616 | tf_op jit(solution)/shard_map/while/body/eval_jaxpr/ppermute | solution.py:23
  107.5 28.5 %collective-permute-start.2 = (bf16[4,512,128]{2,1,0:T(8,128)(2,1)}, bf16[4,512,128]{2,1,0:T(8,128)(2,1)S(1)}, u32[]{:S(2)}, u32[]{:S(2)}) collective-permute-start(bf16[4,512,128]{2,1,0:T(8,128)(2,1)} %get-tuple-element.586), channel_id=1, source_target_pairs={{0,2},{2,4},{4,6},{6,8},{8,10},{10,12},{12,14},{14,16},{16,18},{18... | collective-permute-start | bytes 1572872 | tf_op jit(solution)/shard_map/while/body/eval_jaxpr/ppermute | solution.py:23
  108.5 16.7 %collective-permute-start.3 = (bf16[4,64,128]{2,1,0:T(8,128)(2,1)}, bf16[4,64,128]{2,1,0:T(8,128)(2,1)S(1)}, u32[]{:S(2)}, u32[]{:S(2)}) collective-permute-start(bf16[4,64,128]{2,1,0:T(8,128)(2,1)} %get-tuple-element.584), channel_id=1, source_target_pairs={{0,2},{2,4},{4,6},{6,8},{8,10},{10,12},{12,14},{14,16},{16,18},{18... | collective-permute-start | bytes 196616 | tf_op jit(solution)/shard_map/while/body/eval_jaxpr/ppermute | solution.py:23
  145.2 19.2 %collective-permute-start = (bf16[4,512,128]{2,1,0:T(8,128)(2,1)}, bf16[4,512,128]{2,1,0:T(8,128)(2,1)S(1)}, u32[]{:S(2)}, u32[]{:S(2)}) collective-permute-start(bf16[4,512,128]{2,1,0:T(8,128)(2,1)} %get-tuple-element.585), channel_id=1, source_target_pairs={{0,2},{2,4},{4,6},{6,8},{8,10},{10,12},{12,14},{14,16},{16,18},{18... | collective-permute-start | bytes 1572872 | tf_op jit(solution)/shard_map/while/body/eval_jaxpr/ppermute | solution.py:23
  145.2 12.2 %collective-permute-start.1 = (bf16[4,64,128]{2,1,0:T(8,128)(2,1)S(1)}, bf16[4,64,128]{2,1,0:T(8,128)(2,1)S(1)}, u32[]{:S(2)}, u32[]{:S(2)}) collective-permute-start(bf16[4,64,128]{2,1,0:T(8,128)(2,1)S(1)} %get-tuple-element.583), channel_id=1, source_target_pairs={{0,2},{2,4},{4,6},{6,8},{8,10},{10,12},{12,14},{14,16},{16,18},{18... | collective-permute-start | bytes 196616 | tf_op jit(solution)/shard_map/while/body/eval_jaxpr/ppermute | solution.py:23
  145.2 29.4 %collective-permute-start.2 = (bf16[4,512,128]{2,1,0:T(8,128)(2,1)}, bf16[4,512,128]{2,1,0:T(8,128)(2,1)S(1)}, u32[]{:S(2)}, u32[]{:S(2)}) collective-permute-start(bf16[4,512,128]{2,1,0:T(8,128)(2,1)} %get-tuple-element.586), channel_id=1, source_target_pairs={{0,2},{2,4},{4,6},{6,8},{8,10},{10,12},{12,14},{14,16},{16,18},{18... | collective-permute-start | bytes 1572872 | tf_op jit(solution)/shard_map/while/body/eval_jaxpr/ppermute | solution.py:23
  145.3 18.4 %collective-permute-start.3 = (bf16[4,64,128]{2,1,0:T(8,128)(2,1)}, bf16[4,64,128]{2,1,0:T(8,128)(2,1)S(1)}, u32[]{:S(2)}, u32[]{:S(2)}) collective-permute-start(bf16[4,64,128]{2,1,0:T(8,128)(2,1)} %get-tuple-element.584), channel_id=1, source_target_pairs={{0,2},{2,4},{4,6},{6,8},{8,10},{10,12},{12,14},{14,16},{16,18},{18... | collective-permute-start | bytes 196616 | tf_op jit(solution)/shard_map/while/body/eval_jaxpr/ppermute | solution.py:23
  183.7 19.2 %collective-permute-start = (bf16[4,512,128]{2,1,0:T(8,128)(2,1)}, bf16[4,512,128]{2,1,0:T(8,128)(2,1)S(1)}, u32[]{:S(2)}, u32[]{:S(2)}) collective-permute-start(bf16[4,512,128]{2,1,0:T(8,128)(2,1)} %get-tuple-element.585), channel_id=1, source_target_pairs={{0,2},{2,4},{4,6},{6,8},{8,10},{10,12},{12,14},{14,16},{16,18},{18... | collective-permute-start | bytes 1572872 | tf_op jit(solution)/shard_map/while/body/eval_jaxpr/ppermute | solution.py:23
  183.7 12.2 %collective-permute-start.1 = (bf16[4,64,128]{2,1,0:T(8,128)(2,1)S(1)}, bf16[4,64,128]{2,1,0:T(8,128)(2,1)S(1)}, u32[]{:S(2)}, u32[]{:S(2)}) collective-permute-start(bf16[4,64,128]{2,1,0:T(8,128)(2,1)S(1)} %get-tuple-element.583), channel_id=1, source_target_pairs={{0,2},{2,4},{4,6},{6,8},{8,10},{10,12},{12,14},{14,16},{16,18},{18... | collective-permute-start | bytes 196616 | tf_op jit(solution)/shard_map/while/body/eval_jaxpr/ppermute | solution.py:23
  183.8 29.4 %collective-permute-start.2 = (bf16[4,512,128]{2,1,0:T(8,128)(2,1)}, bf16[4,512,128]{2,1,0:T(8,128)(2,1)S(1)}, u32[]{:S(2)}, u32[]{:S(2)}) collective-permute-start(bf16[4,512,128]{2,1,0:T(8,128)(2,1)} %get-tuple-element.586), channel_id=1, source_target_pairs={{0,2},{2,4},{4,6},{6,8},{8,10},{10,12},{12,14},{14,16},{16,18},{18... | collective-permute-start | bytes 1572872 | tf_op jit(solution)/shard_map/while/body/eval_jaxpr/ppermute | solution.py:23
  183.8 18.4 %collective-permute-start.3 = (bf16[4,64,128]{2,1,0:T(8,128)(2,1)}, bf16[4,64,128]{2,1,0:T(8,128)(2,1)S(1)}, u32[]{:S(2)}, u32[]{:S(2)}) collective-permute-start(bf16[4,64,128]{2,1,0:T(8,128)(2,1)} %get-tuple-element.584), channel_id=1, source_target_pairs={{0,2},{2,4},{4,6},{6,8},{8,10},{10,12},{12,14},{14,16},{16,18},{18... | collective-permute-start | bytes 196616 | tf_op jit(solution)/shard_map/while/body/eval_jaxpr/ppermute | solution.py:23
  222.3 19.2 %collective-permute-start = (bf16[4,512,128]{2,1,0:T(8,128)(2,1)}, bf16[4,512,128]{2,1,0:T(8,128)(2,1)S(1)}, u32[]{:S(2)}, u32[]{:S(2)}) collective-permute-start(bf16[4,512,128]{2,1,0:T(8,128)(2,1)} %get-tuple-element.585), channel_id=1, source_target_pairs={{0,2},{2,4},{4,6},{6,8},{8,10},{10,12},{12,14},{14,16},{16,18},{18... | collective-permute-start | bytes 1572872 | tf_op jit(solution)/shard_map/while/body/eval_jaxpr/ppermute | solution.py:23
  222.3 12.2 %collective-permute-start.1 = (bf16[4,64,128]{2,1,0:T(8,128)(2,1)S(1)}, bf16[4,64,128]{2,1,0:T(8,128)(2,1)S(1)}, u32[]{:S(2)}, u32[]{:S(2)}) collective-permute-start(bf16[4,64,128]{2,1,0:T(8,128)(2,1)S(1)} %get-tuple-element.583), channel_id=1, source_target_pairs={{0,2},{2,4},{4,6},{6,8},{8,10},{10,12},{12,14},{14,16},{16,18},{18... | collective-permute-start | bytes 196616 | tf_op jit(solution)/shard_map/while/body/eval_jaxpr/ppermute | solution.py:23
  222.3 29.4 %collective-permute-start.2 = (bf16[4,512,128]{2,1,0:T(8,128)(2,1)}, bf16[4,512,128]{2,1,0:T(8,128)(2,1)S(1)}, u32[]{:S(2)}, u32[]{:S(2)}) collective-permute-start(bf16[4,512,128]{2,1,0:T(8,128)(2,1)} %get-tuple-element.586), channel_id=1, source_target_pairs={{0,2},{2,4},{4,6},{6,8},{8,10},{10,12},{12,14},{14,16},{16,18},{18... | collective-permute-start | bytes 1572872 | tf_op jit(solution)/shard_map/while/body/eval_jaxpr/ppermute | solution.py:23
  222.4 18.4 %collective-permute-start.3 = (bf16[4,64,128]{2,1,0:T(8,128)(2,1)}, bf16[4,64,128]{2,1,0:T(8,128)(2,1)S(1)}, u32[]{:S(2)}, u32[]{:S(2)}) collective-permute-start(bf16[4,64,128]{2,1,0:T(8,128)(2,1)} %get-tuple-element.584), channel_id=1, source_target_pairs={{0,2},{2,4},{4,6},{6,8},{8,10},{10,12},{12,14},{14,16},{16,18},{18... | collective-permute-start | bytes 196616 | tf_op jit(solution)/shard_map/while/body/eval_jaxpr/ppermute | solution.py:23
  260.8 19.2 %collective-permute-start = (bf16[4,512,128]{2,1,0:T(8,128)(2,1)}, bf16[4,512,128]{2,1,0:T(8,128)(2,1)S(1)}, u32[]{:S(2)}, u32[]{:S(2)}) collective-permute-start(bf16[4,512,128]{2,1,0:T(8,128)(2,1)} %get-tuple-element.585), channel_id=1, source_target_pairs={{0,2},{2,4},{4,6},{6,8},{8,10},{10,12},{12,14},{14,16},{16,18},{18... | collective-permute-start | bytes 1572872 | tf_op jit(solution)/shard_map/while/body/eval_jaxpr/ppermute | solution.py:23
  260.8 12.2 %collective-permute-start.1 = (bf16[4,64,128]{2,1,0:T(8,128)(2,1)S(1)}, bf16[4,64,128]{2,1,0:T(8,128)(2,1)S(1)}, u32[]{:S(2)}, u32[]{:S(2)}) collective-permute-start(bf16[4,64,128]{2,1,0:T(8,128)(2,1)S(1)} %get-tuple-element.583), channel_id=1, source_target_pairs={{0,2},{2,4},{4,6},{6,8},{8,10},{10,12},{12,14},{14,16},{16,18},{18... | collective-permute-start | bytes 196616 | tf_op jit(solution)/shard_map/while/body/eval_jaxpr/ppermute | solution.py:23
  260.9 29.4 %collective-permute-start.2 = (bf16[4,512,128]{2,1,0:T(8,128)(2,1)}, bf16[4,512,128]{2,1,0:T(8,128)(2,1)S(1)}, u32[]{:S(2)}, u32[]{:S(2)}) collective-permute-start(bf16[4,512,128]{2,1,0:T(8,128)(2,1)} %get-tuple-element.586), channel_id=1, source_target_pairs={{0,2},{2,4},{4,6},{6,8},{8,10},{10,12},{12,14},{14,16},{16,18},{18... | collective-permute-start | bytes 1572872 | tf_op jit(solution)/shard_map/while/body/eval_jaxpr/ppermute | solution.py:23
  261.0 18.4 %collective-permute-start.3 = (bf16[4,64,128]{2,1,0:T(8,128)(2,1)}, bf16[4,64,128]{2,1,0:T(8,128)(2,1)S(1)}, u32[]{:S(2)}, u32[]{:S(2)}) collective-permute-start(bf16[4,64,128]{2,1,0:T(8,128)(2,1)} %get-tuple-element.584), channel_id=1, source_target_pairs={{0,2},{2,4},{4,6},{6,8},{8,10},{10,12},{12,14},{14,16},{16,18},{18... | collective-permute-start | bytes 196616 | tf_op jit(solution)/shard_map/while/body/eval_jaxpr/ppermute | solution.py:23
  299.4 19.2 %collective-permute-start = (bf16[4,512,128]{2,1,0:T(8,128)(2,1)}, bf16[4,512,128]{2,1,0:T(8,128)(2,1)S(1)}, u32[]{:S(2)}, u32[]{:S(2)}) collective-permute-start(bf16[4,512,128]{2,1,0:T(8,128)(2,1)} %get-tuple-element.585), channel_id=1, source_target_pairs={{0,2},{2,4},{4,6},{6,8},{8,10},{10,12},{12,14},{14,16},{16,18},{18... | collective-permute-start | bytes 1572872 | tf_op jit(solution)/shard_map/while/body/eval_jaxpr/ppermute | solution.py:23
  299.4 12.2 %collective-permute-start.1 = (bf16[4,64,128]{2,1,0:T(8,128)(2,1)S(1)}, bf16[4,64,128]{2,1,0:T(8,128)(2,1)S(1)}, u32[]{:S(2)}, u32[]{:S(2)}) collective-permute-start(bf16[4,64,128]{2,1,0:T(8,128)(2,1)S(1)} %get-tuple-element.583), channel_id=1, source_target_pairs={{0,2},{2,4},{4,6},{6,8},{8,10},{10,12},{12,14},{14,16},{16,18},{18... | collective-permute-start | bytes 196616 | tf_op jit(solution)/shard_map/while/body/eval_jaxpr/ppermute | solution.py:23
  299.4 29.4 %collective-permute-start.2 = (bf16[4,512,128]{2,1,0:T(8,128)(2,1)}, bf16[4,512,128]{2,1,0:T(8,128)(2,1)S(1)}, u32[]{:S(2)}, u32[]{:S(2)}) collective-permute-start(bf16[4,512,128]{2,1,0:T(8,128)(2,1)} %get-tuple-element.586), channel_id=1, source_target_pairs={{0,2},{2,4},{4,6},{6,8},{8,10},{10,12},{12,14},{14,16},{16,18},{18... | collective-permute-start | bytes 1572872 | tf_op jit(solution)/shard_map/while/body/eval_jaxpr/ppermute | solution.py:23
  299.5 18.4 %collective-permute-start.3 = (bf16[4,64,128]{2,1,0:T(8,128)(2,1)}, bf16[4,64,128]{2,1,0:T(8,128)(2,1)S(1)}, u32[]{:S(2)}, u32[]{:S(2)}) collective-permute-start(bf16[4,64,128]{2,1,0:T(8,128)(2,1)} %get-tuple-element.584), channel_id=1, source_target_pairs={{0,2},{2,4},{4,6},{6,8},{8,10},{10,12},{12,14},{14,16},{16,18},{18... | collective-permute-start | bytes 196616 | tf_op jit(solution)/shard_map/while/body/eval_jaxpr/ppermute | solution.py:23
  337.9 19.2 %collective-permute-start = (bf16[4,512,128]{2,1,0:T(8,128)(2,1)}, bf16[4,512,128]{2,1,0:T(8,128)(2,1)S(1)}, u32[]{:S(2)}, u32[]{:S(2)}) collective-permute-start(bf16[4,512,128]{2,1,0:T(8,128)(2,1)} %get-tuple-element.585), channel_id=1, source_target_pairs={{0,2},{2,4},{4,6},{6,8},{8,10},{10,12},{12,14},{14,16},{16,18},{18... | collective-permute-start | bytes 1572872 | tf_op jit(solution)/shard_map/while/body/eval_jaxpr/ppermute | solution.py:23
  337.9 12.2 %collective-permute-start.1 = (bf16[4,64,128]{2,1,0:T(8,128)(2,1)S(1)}, bf16[4,64,128]{2,1,0:T(8,128)(2,1)S(1)}, u32[]{:S(2)}, u32[]{:S(2)}) collective-permute-start(bf16[4,64,128]{2,1,0:T(8,128)(2,1)S(1)} %get-tuple-element.583), channel_id=1, source_target_pairs={{0,2},{2,4},{4,6},{6,8},{8,10},{10,12},{12,14},{14,16},{16,18},{18... | collective-permute-start | bytes 196616 | tf_op jit(solution)/shard_map/while/body/eval_jaxpr/ppermute | solution.py:23
  338.0 29.4 %collective-permute-start.2 = (bf16[4,512,128]{2,1,0:T(8,128)(2,1)}, bf16[4,512,128]{2,1,0:T(8,128)(2,1)S(1)}, u32[]{:S(2)}, u32[]{:S(2)}) collective-permute-start(bf16[4,512,128]{2,1,0:T(8,128)(2,1)} %get-tuple-element.586), channel_id=1, source_target_pairs={{0,2},{2,4},{4,6},{6,8},{8,10},{10,12},{12,14},{14,16},{16,18},{18... | collective-permute-start | bytes 1572872 | tf_op jit(solution)/shard_map/while/body/eval_jaxpr/ppermute | solution.py:23
  338.1 18.4 %collective-permute-start.3 = (bf16[4,64,128]{2,1,0:T(8,128)(2,1)}, bf16[4,64,128]{2,1,0:T(8,128)(2,1)S(1)}, u32[]{:S(2)}, u32[]{:S(2)}) collective-permute-start(bf16[4,64,128]{2,1,0:T(8,128)(2,1)} %get-tuple-element.584), channel_id=1, source_target_pairs={{0,2},{2,4},{4,6},{6,8},{8,10},{10,12},{12,14},{14,16},{16,18},{18... | collective-permute-start | bytes 196616 | tf_op jit(solution)/shard_map/while/body/eval_jaxpr/ppermute | solution.py:23
  376.5 19.2 %collective-permute-start = (bf16[4,512,128]{2,1,0:T(8,128)(2,1)}, bf16[4,512,128]{2,1,0:T(8,128)(2,1)S(1)}, u32[]{:S(2)}, u32[]{:S(2)}) collective-permute-start(bf16[4,512,128]{2,1,0:T(8,128)(2,1)} %get-tuple-element.585), channel_id=1, source_target_pairs={{0,2},{2,4},{4,6},{6,8},{8,10},{10,12},{12,14},{14,16},{16,18},{18... | collective-permute-start | bytes 1572872 | tf_op jit(solution)/shard_map/while/body/eval_jaxpr/ppermute | solution.py:23
  376.5 12.2 %collective-permute-start.1 = (bf16[4,64,128]{2,1,0:T(8,128)(2,1)S(1)}, bf16[4,64,128]{2,1,0:T(8,128)(2,1)S(1)}, u32[]{:S(2)}, u32[]{:S(2)}) collective-permute-start(bf16[4,64,128]{2,1,0:T(8,128)(2,1)S(1)} %get-tuple-element.583), channel_id=1, source_target_pairs={{0,2},{2,4},{4,6},{6,8},{8,10},{10,12},{12,14},{14,16},{16,18},{18... | collective-permute-start | bytes 196616 | tf_op jit(solution)/shard_map/while/body/eval_jaxpr/ppermute | solution.py:23
  376.5 29.4 %collective-permute-start.2 = (bf16[4,512,128]{2,1,0:T(8,128)(2,1)}, bf16[4,512,128]{2,1,0:T(8,128)(2,1)S(1)}, u32[]{:S(2)}, u32[]{:S(2)}) collective-permute-start(bf16[4,512,128]{2,1,0:T(8,128)(2,1)} %get-tuple-element.586), channel_id=1, source_target_pairs={{0,2},{2,4},{4,6},{6,8},{8,10},{10,12},{12,14},{14,16},{16,18},{18... | collective-permute-start | bytes 1572872 | tf_op jit(solution)/shard_map/while/body/eval_jaxpr/ppermute | solution.py:23
  376.6 18.4 %collective-permute-start.3 = (bf16[4,64,128]{2,1,0:T(8,128)(2,1)}, bf16[4,64,128]{2,1,0:T(8,128)(2,1)S(1)}, u32[]{:S(2)}, u32[]{:S(2)}) collective-permute-start(bf16[4,64,128]{2,1,0:T(8,128)(2,1)} %get-tuple-element.584), channel_id=1, source_target_pairs={{0,2},{2,4},{4,6},{6,8},{8,10},{10,12},{12,14},{14,16},{16,18},{18... | collective-permute-start | bytes 196616 | tf_op jit(solution)/shard_map/while/body/eval_jaxpr/ppermute | solution.py:23
  415.0 19.2 %collective-permute-start = (bf16[4,512,128]{2,1,0:T(8,128)(2,1)}, bf16[4,512,128]{2,1,0:T(8,128)(2,1)S(1)}, u32[]{:S(2)}, u32[]{:S(2)}) collective-permute-start(bf16[4,512,128]{2,1,0:T(8,128)(2,1)} %get-tuple-element.585), channel_id=1, source_target_pairs={{0,2},{2,4},{4,6},{6,8},{8,10},{10,12},{12,14},{14,16},{16,18},{18... | collective-permute-start | bytes 1572872 | tf_op jit(solution)/shard_map/while/body/eval_jaxpr/ppermute | solution.py:23
  415.0 12.2 %collective-permute-start.1 = (bf16[4,64,128]{2,1,0:T(8,128)(2,1)S(1)}, bf16[4,64,128]{2,1,0:T(8,128)(2,1)S(1)}, u32[]{:S(2)}, u32[]{:S(2)}) collective-permute-start(bf16[4,64,128]{2,1,0:T(8,128)(2,1)S(1)} %get-tuple-element.583), channel_id=1, source_target_pairs={{0,2},{2,4},{4,6},{6,8},{8,10},{10,12},{12,14},{14,16},{16,18},{18... | collective-permute-start | bytes 196616 | tf_op jit(solution)/shard_map/while/body/eval_jaxpr/ppermute | solution.py:23
  415.1 29.4 %collective-permute-start.2 = (bf16[4,512,128]{2,1,0:T(8,128)(2,1)}, bf16[4,512,128]{2,1,0:T(8,128)(2,1)S(1)}, u32[]{:S(2)}, u32[]{:S(2)}) collective-permute-start(bf16[4,512,128]{2,1,0:T(8,128)(2,1)} %get-tuple-element.586), channel_id=1, source_target_pairs={{0,2},{2,4},{4,6},{6,8},{8,10},{10,12},{12,14},{14,16},{16,18},{18... | collective-permute-start | bytes 1572872 | tf_op jit(solution)/shard_map/while/body/eval_jaxpr/ppermute | solution.py:23
  415.2 18.4 %collective-permute-start.3 = (bf16[4,64,128]{2,1,0:T(8,128)(2,1)}, bf16[4,64,128]{2,1,0:T(8,128)(2,1)S(1)}, u32[]{:S(2)}, u32[]{:S(2)}) collective-permute-start(bf16[4,64,128]{2,1,0:T(8,128)(2,1)} %get-tuple-element.584), channel_id=1, source_target_pairs={{0,2},{2,4},{4,6},{6,8},{8,10},{10,12},{12,14},{14,16},{16,18},{18... | collective-permute-start | bytes 196616 | tf_op jit(solution)/shard_map/while/body/eval_jaxpr/ppermute | solution.py:23
  453.6 19.2 %collective-permute-start = (bf16[4,512,128]{2,1,0:T(8,128)(2,1)}, bf16[4,512,128]{2,1,0:T(8,128)(2,1)S(1)}, u32[]{:S(2)}, u32[]{:S(2)}) collective-permute-start(bf16[4,512,128]{2,1,0:T(8,128)(2,1)} %get-tuple-element.585), channel_id=1, source_target_pairs={{0,2},{2,4},{4,6},{6,8},{8,10},{10,12},{12,14},{14,16},{16,18},{18... | collective-permute-start | bytes 1572872 | tf_op jit(solution)/shard_map/while/body/eval_jaxpr/ppermute | solution.py:23
  453.6 12.2 %collective-permute-start.1 = (bf16[4,64,128]{2,1,0:T(8,128)(2,1)S(1)}, bf16[4,64,128]{2,1,0:T(8,128)(2,1)S(1)}, u32[]{:S(2)}, u32[]{:S(2)}) collective-permute-start(bf16[4,64,128]{2,1,0:T(8,128)(2,1)S(1)} %get-tuple-element.583), channel_id=1, source_target_pairs={{0,2},{2,4},{4,6},{6,8},{8,10},{10,12},{12,14},{14,16},{16,18},{18... | collective-permute-start | bytes 196616 | tf_op jit(solution)/shard_map/while/body/eval_jaxpr/ppermute | solution.py:23
  453.6 29.4 %collective-permute-start.2 = (bf16[4,512,128]{2,1,0:T(8,128)(2,1)}, bf16[4,512,128]{2,1,0:T(8,128)(2,1)S(1)}, u32[]{:S(2)}, u32[]{:S(2)}) collective-permute-start(bf16[4,512,128]{2,1,0:T(8,128)(2,1)} %get-tuple-element.586), channel_id=1, source_target_pairs={{0,2},{2,4},{4,6},{6,8},{8,10},{10,12},{12,14},{14,16},{16,18},{18... | collective-permute-start | bytes 1572872 | tf_op jit(solution)/shard_map/while/body/eval_jaxpr/ppermute | solution.py:23
  453.7 18.4 %collective-permute-start.3 = (bf16[4,64,128]{2,1,0:T(8,128)(2,1)}, bf16[4,64,128]{2,1,0:T(8,128)(2,1)S(1)}, u32[]{:S(2)}, u32[]{:S(2)}) collective-permute-start(bf16[4,64,128]{2,1,0:T(8,128)(2,1)} %get-tuple-element.584), channel_id=1, source_target_pairs={{0,2},{2,4},{4,6},{6,8},{8,10},{10,12},{12,14},{14,16},{16,18},{18... | collective-permute-start | bytes 196616 | tf_op jit(solution)/shard_map/while/body/eval_jaxpr/ppermute | solution.py:23
  492.1 19.2 %collective-permute-start = (bf16[4,512,128]{2,1,0:T(8,128)(2,1)}, bf16[4,512,128]{2,1,0:T(8,128)(2,1)S(1)}, u32[]{:S(2)}, u32[]{:S(2)}) collective-permute-start(bf16[4,512,128]{2,1,0:T(8,128)(2,1)} %get-tuple-element.585), channel_id=1, source_target_pairs={{0,2},{2,4},{4,6},{6,8},{8,10},{10,12},{12,14},{14,16},{16,18},{18... | collective-permute-start | bytes 1572872 | tf_op jit(solution)/shard_map/while/body/eval_jaxpr/ppermute | solution.py:23
  492.1 12.2 %collective-permute-start.1 = (bf16[4,64,128]{2,1,0:T(8,128)(2,1)S(1)}, bf16[4,64,128]{2,1,0:T(8,128)(2,1)S(1)}, u32[]{:S(2)}, u32[]{:S(2)}) collective-permute-start(bf16[4,64,128]{2,1,0:T(8,128)(2,1)S(1)} %get-tuple-element.583), channel_id=1, source_target_pairs={{0,2},{2,4},{4,6},{6,8},{8,10},{10,12},{12,14},{14,16},{16,18},{18... | collective-permute-start | bytes 196616 | tf_op jit(solution)/shard_map/while/body/eval_jaxpr/ppermute | solution.py:23
  492.2 29.4 %collective-permute-start.2 = (bf16[4,512,128]{2,1,0:T(8,128)(2,1)}, bf16[4,512,128]{2,1,0:T(8,128)(2,1)S(1)}, u32[]{:S(2)}, u32[]{:S(2)}) collective-permute-start(bf16[4,512,128]{2,1,0:T(8,128)(2,1)} %get-tuple-element.586), channel_id=1, source_target_pairs={{0,2},{2,4},{4,6},{6,8},{8,10},{10,12},{12,14},{14,16},{16,18},{18... | collective-permute-start | bytes 1572872 | tf_op jit(solution)/shard_map/while/body/eval_jaxpr/ppermute | solution.py:23
  492.3 18.4 %collective-permute-start.3 = (bf16[4,64,128]{2,1,0:T(8,128)(2,1)}, bf16[4,64,128]{2,1,0:T(8,128)(2,1)S(1)}, u32[]{:S(2)}, u32[]{:S(2)}) collective-permute-start(bf16[4,64,128]{2,1,0:T(8,128)(2,1)} %get-tuple-element.584), channel_id=1, source_target_pairs={{0,2},{2,4},{4,6},{6,8},{8,10},{10,12},{12,14},{14,16},{16,18},{18... | collective-permute-start | bytes 196616 | tf_op jit(solution)/shard_map/while/body/eval_jaxpr/ppermute | solution.py:23
  530.7 19.2 %collective-permute-start = (bf16[4,512,128]{2,1,0:T(8,128)(2,1)}, bf16[4,512,128]{2,1,0:T(8,128)(2,1)S(1)}, u32[]{:S(2)}, u32[]{:S(2)}) collective-permute-start(bf16[4,512,128]{2,1,0:T(8,128)(2,1)} %get-tuple-element.585), channel_id=1, source_target_pairs={{0,2},{2,4},{4,6},{6,8},{8,10},{10,12},{12,14},{14,16},{16,18},{18... | collective-permute-start | bytes 1572872 | tf_op jit(solution)/shard_map/while/body/eval_jaxpr/ppermute | solution.py:23
  530.7 12.2 %collective-permute-start.1 = (bf16[4,64,128]{2,1,0:T(8,128)(2,1)S(1)}, bf16[4,64,128]{2,1,0:T(8,128)(2,1)S(1)}, u32[]{:S(2)}, u32[]{:S(2)}) collective-permute-start(bf16[4,64,128]{2,1,0:T(8,128)(2,1)S(1)} %get-tuple-element.583), channel_id=1, source_target_pairs={{0,2},{2,4},{4,6},{6,8},{8,10},{10,12},{12,14},{14,16},{16,18},{18... | collective-permute-start | bytes 196616 | tf_op jit(solution)/shard_map/while/body/eval_jaxpr/ppermute | solution.py:23
  530.7 29.4 %collective-permute-start.2 = (bf16[4,512,128]{2,1,0:T(8,128)(2,1)}, bf16[4,512,128]{2,1,0:T(8,128)(2,1)S(1)}, u32[]{:S(2)}, u32[]{:S(2)}) collective-permute-start(bf16[4,512,128]{2,1,0:T(8,128)(2,1)} %get-tuple-element.586), channel_id=1, source_target_pairs={{0,2},{2,4},{4,6},{6,8},{8,10},{10,12},{12,14},{14,16},{16,18},{18... | collective-permute-start | bytes 1572872 | tf_op jit(solution)/shard_map/while/body/eval_jaxpr/ppermute | solution.py:23
  530.8 18.4 %collective-permute-start.3 = (bf16[4,64,128]{2,1,0:T(8,128)(2,1)}, bf16[4,64,128]{2,1,0:T(8,128)(2,1)S(1)}, u32[]{:S(2)}, u32[]{:S(2)}) collective-permute-start(bf16[4,64,128]{2,1,0:T(8,128)(2,1)} %get-tuple-element.584), channel_id=1, source_target_pairs={{0,2},{2,4},{4,6},{6,8},{8,10},{10,12},{12,14},{14,16},{16,18},{18... | collective-permute-start | bytes 196616 | tf_op jit(solution)/shard_map/while/body/eval_jaxpr/ppermute | solution.py:23
  569.2 19.2 %collective-permute-start = (bf16[4,512,128]{2,1,0:T(8,128)(2,1)}, bf16[4,512,128]{2,1,0:T(8,128)(2,1)S(1)}, u32[]{:S(2)}, u32[]{:S(2)}) collective-permute-start(bf16[4,512,128]{2,1,0:T(8,128)(2,1)} %get-tuple-element.585), channel_id=1, source_target_pairs={{0,2},{2,4},{4,6},{6,8},{8,10},{10,12},{12,14},{14,16},{16,18},{18... | collective-permute-start | bytes 1572872 | tf_op jit(solution)/shard_map/while/body/eval_jaxpr/ppermute | solution.py:23
  569.2 12.2 %collective-permute-start.1 = (bf16[4,64,128]{2,1,0:T(8,128)(2,1)S(1)}, bf16[4,64,128]{2,1,0:T(8,128)(2,1)S(1)}, u32[]{:S(2)}, u32[]{:S(2)}) collective-permute-start(bf16[4,64,128]{2,1,0:T(8,128)(2,1)S(1)} %get-tuple-element.583), channel_id=1, source_target_pairs={{0,2},{2,4},{4,6},{6,8},{8,10},{10,12},{12,14},{14,16},{16,18},{18... | collective-permute-start | bytes 196616 | tf_op jit(solution)/shard_map/while/body/eval_jaxpr/ppermute | solution.py:23
  569.3 29.4 %collective-permute-start.2 = (bf16[4,512,128]{2,1,0:T(8,128)(2,1)}, bf16[4,512,128]{2,1,0:T(8,128)(2,1)S(1)}, u32[]{:S(2)}, u32[]{:S(2)}) collective-permute-start(bf16[4,512,128]{2,1,0:T(8,128)(2,1)} %get-tuple-element.586), channel_id=1, source_target_pairs={{0,2},{2,4},{4,6},{6,8},{8,10},{10,12},{12,14},{14,16},{16,18},{18... | collective-permute-start | bytes 1572872 | tf_op jit(solution)/shard_map/while/body/eval_jaxpr/ppermute | solution.py:23
  569.4 18.4 %collective-permute-start.3 = (bf16[4,64,128]{2,1,0:T(8,128)(2,1)}, bf16[4,64,128]{2,1,0:T(8,128)(2,1)S(1)}, u32[]{:S(2)}, u32[]{:S(2)}) collective-permute-start(bf16[4,64,128]{2,1,0:T(8,128)(2,1)} %get-tuple-element.584), channel_id=1, source_target_pairs={{0,2},{2,4},{4,6},{6,8},{8,10},{10,12},{12,14},{14,16},{16,18},{18... | collective-permute-start | bytes 196616 | tf_op jit(solution)/shard_map/while/body/eval_jaxpr/ppermute | solution.py:23
  607.8 19.2 %collective-permute-start = (bf16[4,512,128]{2,1,0:T(8,128)(2,1)}, bf16[4,512,128]{2,1,0:T(8,128)(2,1)S(1)}, u32[]{:S(2)}, u32[]{:S(2)}) collective-permute-start(bf16[4,512,128]{2,1,0:T(8,128)(2,1)} %get-tuple-element.585), channel_id=1, source_target_pairs={{0,2},{2,4},{4,6},{6,8},{8,10},{10,12},{12,14},{14,16},{16,18},{18... | collective-permute-start | bytes 1572872 | tf_op jit(solution)/shard_map/while/body/eval_jaxpr/ppermute | solution.py:23
  607.8 12.2 %collective-permute-start.1 = (bf16[4,64,128]{2,1,0:T(8,128)(2,1)S(1)}, bf16[4,64,128]{2,1,0:T(8,128)(2,1)S(1)}, u32[]{:S(2)}, u32[]{:S(2)}) collective-permute-start(bf16[4,64,128]{2,1,0:T(8,128)(2,1)S(1)} %get-tuple-element.583), channel_id=1, source_target_pairs={{0,2},{2,4},{4,6},{6,8},{8,10},{10,12},{12,14},{14,16},{16,18},{18... | collective-permute-start | bytes 196616 | tf_op jit(solution)/shard_map/while/body/eval_jaxpr/ppermute | solution.py:23
  607.9 29.4 %collective-permute-start.2 = (bf16[4,512,128]{2,1,0:T(8,128)(2,1)}, bf16[4,512,128]{2,1,0:T(8,128)(2,1)S(1)}, u32[]{:S(2)}, u32[]{:S(2)}) collective-permute-start(bf16[4,512,128]{2,1,0:T(8,128)(2,1)} %get-tuple-element.586), channel_id=1, source_target_pairs={{0,2},{2,4},{4,6},{6,8},{8,10},{10,12},{12,14},{14,16},{16,18},{18... | collective-permute-start | bytes 1572872 | tf_op jit(solution)/shard_map/while/body/eval_jaxpr/ppermute | solution.py:23
  607.9 18.4 %collective-permute-start.3 = (bf16[4,64,128]{2,1,0:T(8,128)(2,1)}, bf16[4,64,128]{2,1,0:T(8,128)(2,1)S(1)}, u32[]{:S(2)}, u32[]{:S(2)}) collective-permute-start(bf16[4,64,128]{2,1,0:T(8,128)(2,1)} %get-tuple-element.584), channel_id=1, source_target_pairs={{0,2},{2,4},{4,6},{6,8},{8,10},{10,12},{12,14},{14,16},{16,18},{18... | collective-permute-start | bytes 196616 | tf_op jit(solution)/shard_map/while/body/eval_jaxpr/ppermute | solution.py:23
  646.3 19.2 %collective-permute-start = (bf16[4,512,128]{2,1,0:T(8,128)(2,1)}, bf16[4,512,128]{2,1,0:T(8,128)(2,1)S(1)}, u32[]{:S(2)}, u32[]{:S(2)}) collective-permute-start(bf16[4,512,128]{2,1,0:T(8,128)(2,1)} %get-tuple-element.585), channel_id=1, source_target_pairs={{0,2},{2,4},{4,6},{6,8},{8,10},{10,12},{12,14},{14,16},{16,18},{18... | collective-permute-start | bytes 1572872 | tf_op jit(solution)/shard_map/while/body/eval_jaxpr/ppermute | solution.py:23
  646.3 12.2 %collective-permute-start.1 = (bf16[4,64,128]{2,1,0:T(8,128)(2,1)S(1)}, bf16[4,64,128]{2,1,0:T(8,128)(2,1)S(1)}, u32[]{:S(2)}, u32[]{:S(2)}) collective-permute-start(bf16[4,64,128]{2,1,0:T(8,128)(2,1)S(1)} %get-tuple-element.583), channel_id=1, source_target_pairs={{0,2},{2,4},{4,6},{6,8},{8,10},{10,12},{12,14},{14,16},{16,18},{18... | collective-permute-start | bytes 196616 | tf_op jit(solution)/shard_map/while/body/eval_jaxpr/ppermute | solution.py:23
  646.4 29.4 %collective-permute-start.2 = (bf16[4,512,128]{2,1,0:T(8,128)(2,1)}, bf16[4,512,128]{2,1,0:T(8,128)(2,1)S(1)}, u32[]{:S(2)}, u32[]{:S(2)}) collective-permute-start(bf16[4,512,128]{2,1,0:T(8,128)(2,1)} %get-tuple-element.586), channel_id=1, source_target_pairs={{0,2},{2,4},{4,6},{6,8},{8,10},{10,12},{12,14},{14,16},{16,18},{18... | collective-permute-start | bytes 1572872 | tf_op jit(solution)/shard_map/while/body/eval_jaxpr/ppermute | solution.py:23
  646.5 18.4 %collective-permute-start.3 = (bf16[4,64,128]{2,1,0:T(8,128)(2,1)}, bf16[4,64,128]{2,1,0:T(8,128)(2,1)S(1)}, u32[]{:S(2)}, u32[]{:S(2)}) collective-permute-start(bf16[4,64,128]{2,1,0:T(8,128)(2,1)} %get-tuple-element.584), channel_id=1, source_target_pairs={{0,2},{2,4},{4,6},{6,8},{8,10},{10,12},{12,14},{14,16},{16,18},{18... | collective-permute-start | bytes 196616 | tf_op jit(solution)/shard_map/while/body/eval_jaxpr/ppermute | solution.py:23
  (50 other events, 260.2 us)
where the time goes:
time: 691 us; the launch traced here: 689 us
  waiting for transfers between devices  256 us (37%)
  matrix products  182 us (26%)
  other arithmetic  118 us (17%)
  local copies, waits for them, and re-layouts  84.8 us (12%)
  starting transfers between devices  33.8 us (5%)
  loops' own time  12.2 us (2%)
    ppermute x60, waiting for transfers between devices, shifted(): return lax.ppermute(value, axis, pairs)  217 us
    dot_general x32, matrix products, attend_piece(): jnp.einsum('hqk,hkd->hqd', rounded, values, preferred_element_type=jnp.fl...  101 us
    dot_general x32, matrix products, attend_piece(): jnp.einsum('hqd,hkd->hqk', queries, keys, preferred_element_type=jnp.floa...  81.5 us
    reduce_sum x32, other arithmetic, attend_piece(): total = factor * total + jnp.sum(weights, axis=-1)  74.6 us
    while x165, local copies, waits for them, and re-layouts  44.8 us
    add x16, other arithmetic, attend_piece(): factor[..., None] * summed  26.8 us
    all_to_all x1, waiting for transfers between devices, shards(): lax.all_to_all(arrange(q_local), 'cp', split_axis=0, concat_axis=0, tiled...  15.5 us
  transfers between devices with their start and end apart: 66, of which 36 were waited for; matrix products, arithmetic and copies ran while one was open for 32% of the time, Pallas kernels for 0%

commit v1 on v0

v1 whole, which is shorter than its diff:
```python
import functools
import math

import jax
import jax.numpy as jnp
from jax import lax
from jax.experimental import pallas as pl
from jax.experimental.pallas import tpu as pltpu
from jax.sharding import PartitionSpec as P

HEAD_SIZE = 128
NEG = -1e30
EXPONENT = HEAD_SIZE ** (-0.5) * math.log2(math.e)


def attend_kernel(
    dims,
    plen_ref,
    q_ref,
    nat_ref,
    fresh_k,
    fresh_v,
    cache_k,
    cache_v,
    out_ref,
    m_ref,
    l_ref,
    acc_ref,
):
    per_step, chunk, fresh_chunk = dims
    rows = q_ref.shape[0]
    slots = cache_k.shape[0]
    plen = plen_ref[0]

    def piece(g, k, v, mask, first):
        q = q_ref[:, g * HEAD_SIZE : (g + 1) * HEAD_SIZE]
        s = lax.dot_general(q, k, (((1,), (1,)), ((), ())), preferred_element_type=jnp.float32)
        if mask is not None:
            s = jnp.where(mask, s, NEG)
        top = jnp.max(s, axis=1, keepdims=True)
        if first:
            m_new = jnp.broadcast_to(top, (rows, HEAD_SIZE))
        else:
            m_old = m_ref[g]
            m_new = jnp.maximum(m_old, top)
        p = jnp.exp2((s - m_new[:, :1]) * EXPONENT)
        part = p[:, :HEAD_SIZE]
        for c in range(1, p.shape[1] // HEAD_SIZE):
            part = part + p[:, c * HEAD_SIZE : (c + 1) * HEAD_SIZE]
        o = jnp.dot(p.astype(jnp.bfloat16), v, preferred_element_type=jnp.float32)
        m_ref[g] = m_new
        if first:
            l_ref[g] = part
            acc_ref[g] = o
        else:
            f = jnp.exp2((m_old - m_new) * EXPONENT)
            l_ref[g] = f * l_ref[g] + part
            acc_ref[g] = f * acc_ref[g] + o

    fresh = fresh_k.shape[0]
    for c in range(fresh // fresh_chunk):
        k = fresh_k[c * fresh_chunk : (c + 1) * fresh_chunk, :]
        v = fresh_v[c * fresh_chunk : (c + 1) * fresh_chunk, :]
        index = c * fresh_chunk + lax.broadcasted_iota(jnp.int32, (rows, fresh_chunk), 1)
        mask = index <= nat_ref[:, :1]
        for g in range(per_step):
            piece(g, k, v, mask, c == 0)

    def body(b, _):
        at = pl.multiple_of(b * chunk, chunk)
        k = cache_k[pl.ds(at, chunk), :]
        v = cache_v[pl.ds(at, chunk), :]
        for g in range(per_step):
            piece(g, k, v, None, False)
        return 0

    full = plen // chunk
    lax.fori_loop(0, full, body, 0)

    @pl.when(full * chunk < plen)
    def _():
        at = pl.multiple_of(full * chunk, chunk)
        k = cache_k[pl.ds(at, chunk), :]
        v = cache_v[pl.ds(at, chunk), :]
        index = at + lax.broadcasted_iota(jnp.int32, (1, chunk), 1)
        for g in range(per_step):
            piece(g, k, v, index < plen, False)

    for g in range(per_step):
        total = jnp.sum(l_ref[g], axis=1, keepdims=True)
        out_ref[:, g * HEAD_SIZE : (g + 1) * HEAD_SIZE] = (acc_ref[g] / total).astype(out_ref.dtype)


def attend(q, nat, fresh_k, fresh_v, cache_k, cache_v, prefix_len, per_step=4, chunk=1024):
    rows, columns = q.shape
    width = per_step * HEAD_SIZE
    fresh, slots = fresh_k.shape[0], cache_k.shape[0]
    whole = lambda i, *_: (0, 0)
    flops = 4 * rows * columns * (fresh + slots)
    return pl.pallas_call(
        functools.partial(attend_kernel, (per_step, min(chunk, slots), min(chunk, fresh))),
        out_shape=jax.ShapeDtypeStruct((rows, columns), jnp.bfloat16),
        grid_spec=pltpu.PrefetchScalarGridSpec(
            num_scalar_prefetch=1,
            grid=(columns // width,),
            in_specs=[
                pl.BlockSpec((rows, width), lambda i, *_: (0, i)),
                pl.BlockSpec((rows, HEAD_SIZE), whole),
                pl.BlockSpec((fresh, HEAD_SIZE), whole),
                pl.BlockSpec((fresh, HEAD_SIZE), whole),
                pl.BlockSpec((slots, HEAD_SIZE), whole),
                pl.BlockSpec((slots, HEAD_SIZE), whole),
            ],
            out_specs=pl.BlockSpec((rows, width), lambda i, *_: (0, i)),
            scratch_shapes=[pltpu.VMEM((per_step, rows, HEAD_SIZE), jnp.float32)] * 3,
        ),
        compiler_params=pltpu.CompilerParams(vmem_limit_bytes=56 * 1024 * 1024),
        cost_estimate=pl.CostEstimate(
            flops=flops, bytes_accessed=4 * fresh * columns, transcendentals=0
        ),
    )(prefix_len, q, nat, fresh_k, fresh_v, cache_k, cache_v)


def shards(
    query,
    fresh_key_rows,
    fresh_value_rows,
    cached_key_rows,
    cached_value_rows,
    prefix_len,
    stripe_owner,
):
    parts = lax.axis_size("cp")
    tps = lax.axis_size("tp")
    me = lax.axis_index("cp")
    heads = cached_key_rows.shape[1] // HEAD_SIZE
    ranks = parts // heads
    q_columns = query.shape[1] // tps // heads
    columns = [[h * ranks + r for h in range(heads)] for r in range(ranks)]
    lines = [[h * ranks + r for r in range(ranks)] for h in range(heads)]

    order = jnp.arange(parts, dtype=jnp.int32)
    inverse = jnp.sum(jnp.where(stripe_owner[None, :] == order[:, None], order[None, :], 0), axis=1)

    def split_heads(array):
        if heads == 1:
            return array
        return lax.all_to_all(
            array, "cp", split_axis=1, concat_axis=0, axis_index_groups=columns, tiled=True
        )

    def collect(array):
        block = array.shape[0]
        mine = split_heads(array)
        everything = lax.all_gather(mine, "cp", axis_index_groups=lines, tiled=True)
        return (
            everything.reshape(ranks, heads, block, HEAD_SIZE)
            .transpose(1, 0, 2, 3)
            .reshape(parts * block, HEAD_SIZE)
        )

    q_local = lax.all_to_all(query, "tp", split_axis=1, concat_axis=0, tiled=True)
    fresh = jnp.concatenate(
        [
            fresh_key_rows.reshape(-1, tps, heads, 1, HEAD_SIZE),
            fresh_value_rows.reshape(-1, tps, heads, 1, HEAD_SIZE),
        ],
        axis=3,
    ).reshape(fresh_key_rows.shape[0], -1)
    f_local = lax.all_to_all(fresh, "tp", split_axis=1, concat_axis=0, tiled=True)
    rows = q_local.shape[0]
    stripe = rows // parts

    by_rank = inverse.reshape(heads, ranks).T.reshape(-1)
    wanted = (by_rank[:, None] * stripe + jnp.arange(stripe, dtype=jnp.int32)[None, :]).reshape(-1)
    pick = (wanted[:, None] == jnp.arange(rows, dtype=jnp.int32)[None, :]).astype(jnp.bfloat16)
    q_sorted = jnp.dot(pick, q_local, preferred_element_type=jnp.float32).astype(jnp.bfloat16)
    q_out = (
        q_sorted.reshape(ranks, heads * stripe, heads, q_columns)
        .transpose(2, 0, 1, 3)
        .reshape(parts * heads * stripe, q_columns)
    )
    q_mine = lax.all_to_all(q_out, "cp", split_axis=0, concat_axis=0, tiled=True)

    cache_k = collect(cached_key_rows)
    cache_v = collect(cached_value_rows)
    if heads > 1:
        f_mine = lax.all_to_all(
            f_local, "cp", split_axis=1, concat_axis=0, axis_index_groups=columns, tiled=True
        )
    else:
        f_mine = f_local
    f_all = lax.all_gather(f_mine, "cp", axis_index_groups=lines, tiled=True)
    f_all = (
        f_all.reshape(ranks, heads, rows, 2 * HEAD_SIZE)
        .transpose(1, 0, 2, 3)
        .reshape(parts * rows, 2 * HEAD_SIZE)
    )
    fresh_k, fresh_v = f_all[:, :HEAD_SIZE], f_all[:, HEAD_SIZE:]

    rank = me % ranks
    residues = jnp.take(by_rank.reshape(ranks, heads), rank, axis=0)
    nat = (
        jnp.arange(parts, dtype=jnp.int32)[:, None, None] * rows
        + residues[None, :, None] * stripe
        + jnp.arange(stripe, dtype=jnp.int32)[None, None, :]
    ).reshape(-1, 1)
    nat = jnp.broadcast_to(nat, (nat.shape[0], HEAD_SIZE))

    done = attend(q_mine, nat, fresh_k, fresh_v, cache_k, cache_v, prefix_len)
    done = (
        done.reshape(parts, heads, stripe, q_columns)
        .transpose(1, 0, 2, 3)
        .reshape(heads * rows, q_columns)
    )
    if heads == 1:
        return done
    return lax.all_to_all(
        done, "cp", split_axis=0, concat_axis=1, axis_index_groups=columns, tiled=True
    )


def solution(mesh):
    return jax.shard_map(
        shards,
        mesh=mesh,
        in_specs=(
            P(("cp", "tp"), None),
            P(("cp", "tp"), None),
            P(("cp", "tp"), None),
            P("cp", "tp"),
            P("cp", "tp"),
            P(),
            P(),
        ),
        out_specs=P("cp", "tp"),
        check_vma=False,
    )
```

time: 691 us -> 234 us (0.34)
  waiting for transfers between devices: 256 us -> 18.2 us
  matrix products: 182 us -> 0.48 us
  other arithmetic: 118 us -> 0.85 us
  Pallas kernels: 0 us -> 82.5 us
  blocking collectives: 0 us -> 82 us
  local copies, waits for them, and re-layouts: 84.8 us -> 21.2 us
  starting transfers between devices: 33.8 us -> 14.3 us
  between operations: 1.48 us -> 14.3 us
  loops' own time: 12.2 us -> 0 us
    ppermute x60 -> x0, waiting for transfers between devices: 217 us -> none  [shifted(): return lax.ppermute(value, axis, pairs)]
    dot_general x64 -> x1, matrix products: 182 us -> 0.48 us  [shards(): jnp.dot(pick, q_local, preferred_element_type=jnp.float32)]
    pallas_call x0 -> x1, Pallas kernels: none -> 82.5 us  [attend(): pl.pallas_call(functools.partial(attend_kernel, (per_step, min(chunk, slo...]
    reduce_sum x32 -> x0, other arithmetic: 74.6 us -> none  [attend_piece(): total = factor * total + jnp.sum(weights, axis=-1)]
    all_to_all x0 -> x3, blocking collectives: none -> 68.9 us  [the longest x2 37.4 us: split_heads(): lax.all_to_all(array, 'cp', split_axis=1, concat_axis=0, axis_index_group...]
    while x165 -> x0, local copies, waits for them, and re-layouts: 44.8 us -> none
    add x63 -> x3, other arithmetic: 27.5 us -> 0.23 us  [the longest x2 0.16 us: shards(): jnp.arange(parts, dtype=jnp.int32)[:, None, None] * rows]
    all_to_all x5 -> x3, waiting for transfers between devices: 29.6 us -> 8.02 us  [the longest x1 3.39 us: shards(): lax.all_to_all(fresh, 'tp', split_axis=1, concat_axis=0, tiled=True)]
  transfers between devices with their start and end apart: 66 -> 6, of which waited for: 36 -> 4; matrix products, arithmetic and copies ran while one was open for 32% -> 6% of each run, Pallas kernels for 0% -> 0%
where the time goes in v1:
time: 234 us
  Pallas kernels  82.5 us (35%)
  blocking collectives  82 us (35%)
  local copies, waits for them, and re-layouts  21.2 us (9%)
  waiting for transfers between devices  18.2 us (8%)
  starting transfers between devices  14.3 us (6%)
  between operations  14.3 us (6%)
    pallas_call x1, Pallas kernels, attend(): pl.pallas_call(functools.partial(attend_kernel, (per_step, min(chunk, slo...  82.5 us
    all_to_all x2, blocking collectives, split_heads(): lax.all_to_all(array, 'cp', split_axis=1, concat_axis=0, axis_index_group...  37.4 us
    all_to_all x1, blocking collectives, shards(): lax.all_to_all(done, 'cp', split_axis=0, concat_axis=1, axis_index_groups...  31.6 us
    all_gather x1, blocking collectives, shards(): f_all = lax.all_gather(f_mine, 'cp', axis_index_groups=lines, tiled=True)  13.1 us
    all_to_all x1, waiting for transfers between devices, shards(): lax.all_to_all(query, 'tp', split_axis=1, concat_axis=0, tiled=True)  10.1 us
    transpose x2, local copies, waits for them, and re-layouts, collect(): return everything.reshape(ranks, heads, block, HEAD_SIZE).transpose(1, 0,...  6.24 us
  transfers between devices with their start and end apart: 6, of which 4 were waited for; matrix products, arithmetic and copies ran while one was open for 6% of the time, Pallas kernels for 0%

profile of v1, /device:TPU:0, one launch (start us, length us, event | category | flops | bytes accessed | tf_op | source)
XLA Modules:
  0.0 233.8 jit_solution(5756384063137649967)
XLA Ops:
  6.5 0.0 copy-start.2
  6.5 0.0 all-gather.3.cloned.1.call-start
  6.5 1.3 copy.71
  7.9 20.6 %all_to_all.122 = bf16[512,4,128]{0,2,1:T(8,128)(2,1)S(1)} all-to-all(bf16[512,4,128]{0,2,1:T(8,128)(2,1)S(1)} %bitcast.57), channel_id=1, replica_groups={{0,8,16,24},{2,10,18,26},{4,12,20,28},{6,14,22,30},{1,9,17,25},{3,11,19..., dimensions={1} | all-to-all | bytes 1048576 | tf_op jit(solution)/shard_map/all_to_all | solution.py:148
  28.5 1.0 copy.72
  29.5 0.0 copy-start.3
  29.5 0.0 all-gather.3.cloned.1.call-update
  29.5 0.0 copy-start.4
  29.5 0.0 all-gather.5.cloned.1.call-start
  29.6 0.0 copy-done.2
  29.6 0.2 copy.74
  29.8 0.0 copy-start
  29.8 16.7 %all_to_all.123 = bf16[512,4,128]{0,2,1:T(8,128)(2,1)S(1)} all-to-all(bf16[512,4,128]{0,2,1:T(8,128)(2,1)S(1)} %bitcast.58), channel_id=1, replica_groups={{0,8,16,24},{2,10,18,26},{4,12,20,28},{6,14,22,30},{1,9,17,25},{3,11,19..., dimensions={1} | all-to-all | bytes 1048576 | tf_op jit(solution)/shard_map/all_to_all | solution.py:148
  46.5 1.0 copy.75
  47.6 0.0 all-gather.5.cloned.1.call-update
  47.6 0.0 copy-done.3
  47.6 0.1 copy.67
  47.7 0.0 copy-done.4
  47.8 0.1 copy.68
  47.9 0.3 pad_maximum_fusion
  48.2 0.7 all_to_all.96
  48.9 3.4 %all-to-all-start.2 = ((bf16[32,2,1024]{2,0,1:T(8,128)(2,1)}), bf16[32,2,1024]{2,0,1:T(8,128)(2,1)S(1)}, u32[]{:S(2)}, u32[]{:S(2)}) async-start(bf16[32,2,1024]{2,0,1:T(8,128)(2,1)} %all_to_all.96), calls=%async_computation.2 | async-start | bytes 262144 | tf_op jit(solution)/shard_map/all_to_all | solution.py:170
  52.3 0.0 copy-done
  52.3 0.0 copy-start.5
  52.3 1.0 copy.83
  53.4 3.4 %all-to-all-done.2 = bf16[32,2,1024]{2,0,1:T(8,128)(2,1)S(1)} async-done(((bf16[32,2,1024]{2,0,1:T(8,128)(2,1)}), bf16[32,2,1024]{2,0,1:T(8,128)(2,1)S(1)}, u32[]{:S(2)}, u32[]{:S(2)}) %all-to-all-start.2) | async-done | bytes 131104 | tf_op jit(solution)/shard_map/all_to_all | solution.py:170
  56.8 3.6 %all-to-all-start = ((bf16[32,2,8192]{2,0,1:T(8,128)(2,1)}), bf16[32,2,8192]{2,0,1:T(8,128)(2,1)S(1)}, u32[]{:S(2)}, u32[]{:S(2)}) async-start(bf16[32,2,8192]{2,0,1:T(8,128)(2,1)} %bitcast.42), calls=%async_computation | async-start | bytes 2097152 | tf_op jit(solution)/shard_map/all_to_all | solution.py:162
  60.4 0.0 copy-done.5
  60.4 0.1 select_reduce_fusion
  60.5 0.1 reshape.142
  60.6 0.1 copy.64
  60.7 0.1 mul.28
  60.8 0.1 iota_add_fusion.1
  60.9 0.1 add.69
  61.0 0.1 all_to_all.99
  61.1 0.7 copy.69
  61.7 10.1 %all-to-all-done = bf16[32,2,8192]{2,0,1:T(8,128)(2,1)S(1)} async-done(((bf16[32,2,8192]{2,0,1:T(8,128)(2,1)}), bf16[32,2,8192]{2,0,1:T(8,128)(2,1)S(1)}, u32[]{:S(2)}, u32[]{:S(2)}) %all-to-all-start) | async-done | bytes 1048608 | tf_op jit(solution)/shard_map/all_to_all | solution.py:162
  71.9 3.5 %all-to-all-start.3 = ((bf16[64,4,256]{2,0,1:T(8,128)(2,1)}), bf16[64,4,256]{2,0,1:T(8,128)(2,1)S(1)}, u32[]{:S(2)}, u32[]{:S(2)}) async-start(bf16[64,4,256]{2,0,1:T(8,128)(2,1)} %copy.69), calls=%async_computation.3 | async-start | bytes 262144 | tf_op jit(solution)/shard_map/all_to_all | solution.py:188
  75.4 0.5 convolution_convert_fusion
  75.9 0.8 reshape.143
  76.7 1.5 copy.66
  78.2 3.1 %all-to-all-done.3 = bf16[64,4,256]{2,0,1:T(8,128)(2,1)S(1)} async-done(((bf16[64,4,256]{2,0,1:T(8,128)(2,1)}), bf16[64,4,256]{2,0,1:T(8,128)(2,1)S(1)}, u32[]{:S(2)}, u32[]{:S(2)}) %all-to-all-start.3) | async-done | bytes 131104 | tf_op jit(solution)/shard_map/all_to_all | solution.py:188
  81.3 3.7 %all-to-all-start.1 = ((bf16[16,16,2048]{2,1,0:T(8,128)(2,1)}), bf16[16,16,2048]{2,1,0:T(8,128)(2,1)S(1)}, u32[]{:S(2)}, u32[]{:S(2)}) async-start(bf16[16,16,2048]{2,1,0:T(8,128)(2,1)} %bitcast.4), calls=%async_computation.1 | async-start | bytes 2097152 | tf_op jit(solution)/shard_map/all_to_all | solution.py:183
  85.7 0.2 multiply_reduce_fusion
  85.9 0.1 broadcast_add_fusion
  86.0 0.1 iota_add_fusion
  86.0 0.1 add.78
  86.2 13.1 %all_gather.9 = bf16[1024,256]{1,0:T(8,128)(2,1)S(1)} all-gather(bf16[256,256]{1,0:T(8,128)(2,1)S(1)} %bitcast.61), channel_id=1, replica_groups={{0,2,4,6},{8,10,12,14},{16,18,20,22},{24,26,28,30},{1,3,5,7},{9,11,13,1..., dimensions={0}, use_global_device_ids=true | all-gather | bytes 655360 | tf_op jit(solution)/shard_map/all_gather | solution.py:193
  99.3 0.8 fusion.1
  100.1 0.0 all-gather.3.cloned.1.call-done
  100.1 3.1 %copy.73 = bf16[4,4,512,128]{3,2,1,0:T(8,128)(2,1)} copy(bf16[4,4,512,128]{3,2,0,1:T(8,128)(2,1)} %bitcast.48) | data formatting | bytes 4194304 | tf_op jit(solution)/shard_map/transpose | solution.py:158
  103.2 0.0 all-gather.5.cloned.1.call-done
  103.3 3.1 %copy.76 = bf16[4,4,512,128]{3,2,1,0:T(8,128)(2,1)} copy(bf16[4,4,512,128]{3,2,0,1:T(8,128)(2,1)} %bitcast.49) | data formatting | bytes 4194304 | tf_op jit(solution)/shard_map/transpose | solution.py:158
  106.4 1.6 all-to-all-done.1
  107.9 0.0 copy-start.1
  107.9 0.9 broadcast_in_dim.37.nat_ref
  108.8 0.1 copy-done.1
  108.9 82.5 %shard_map.73 = bf16[256,2048]{1,0:T(8,128)(2,1)} custom-call(s32[1]{0:T(128)S(6)} %copy.84.plen_ref, bf16[256,2048]{1,0:T(8,128)(2,1)} %bitcast.60, s32[256,128]{1,0:T(8,128)} %broadcast_in_dim.37.nat_ref, bf16[1024,128]{1,0:T(8,128)(2,1)} %get-tuple-element.17.fresh_k, bf16[1024,128]{1,0:T(8,128)(2,1)} %get-tuple-element.16.fresh_v, ...), custom_call_target="tpu_custom_call" | custom-call | flops 19327352832 | bytes 8388608 | tf_op jit(solution)/shard_map/pallas_call | solution.py:100
  191.4 1.5 reshape.152
  192.8 0.9 copy.77
  193.7 0.6 copy.78
  194.3 31.6 %all_to_all.124 = bf16[4,64,2048]{2,1,0:T(8,128)(2,1)S(1)} all-to-all(bf16[4,64,2048]{2,1,0:T(8,128)(2,1)S(1)} %copy.78), channel_id=1, replica_groups={{0,8,16,24},{2,10,18,26},{4,12,20,28},{6,14,22,30},{1,9,17,25},{3,11,19..., dimensions={0} | all-to-all | bytes 2097152 | tf_op jit(solution)/shard_map/all_to_all | solution.py:218
  225.9 1.0 copy.81
  (5 shorter events, 0.1 us)
Async XLA Ops:
  6.5 23.0 %copy-start.2 = (bf16[512,512]{1,0:T(8,128)(2,1)S(1)}, bf16[512,512]{1,0:T(8,128)(2,1)}, u32[]{:S(2)}) copy-start(bf16[512,512]{1,0:T(8,128)(2,1)} %param.11) | copy-start | bytes 1572868
  6.5 93.6 %all-gather.3.cloned.1.call-start = ((), (), s32[]{:S(2)}) async-start(), calls=%async_computation.7 | async-start | bytes 2621440 | tf_op jit(solution)/shard_map/all_gather | solution.py:155
  29.5 18.1 %copy-start.3 = (bf16[32,1024]{1,0:T(8,128)(2,1)S(1)}, bf16[32,1024]{1,0:T(8,128)(2,1)}, u32[]{:S(2)}) copy-start(bf16[32,1024]{1,0:T(8,128)(2,1)} %param.8) | copy-start | bytes 196612
  29.5 18.2 %copy-start.4 = (bf16[32,1024]{1,0:T(8,128)(2,1)S(1)}, bf16[32,1024]{1,0:T(8,128)(2,1)}, u32[]{:S(2)}) copy-start(bf16[32,1024]{1,0:T(8,128)(2,1)} %param.9) | copy-start | bytes 196612
  29.5 73.7 %all-gather.5.cloned.1.call-start = ((), (), s32[]{:S(2)}) async-start(), calls=%async_computation.8 | async-start | bytes 2621440 | tf_op jit(solution)/shard_map/all_gather | solution.py:155
  29.8 22.5 %copy-start = (bf16[32,16384]{1,0:T(8,128)(2,1)S(1)}, bf16[32,16384]{1,0:T(8,128)(2,1)}, u32[]{:S(2)}) copy-start(bf16[32,16384]{1,0:T(8,128)(2,1)} %param.7) | copy-start | bytes 3145732
  48.9 7.8 %all-to-all-start.2 = ((bf16[32,2,1024]{2,0,1:T(8,128)(2,1)}), bf16[32,2,1024]{2,0,1:T(8,128)(2,1)S(1)}, u32[]{:S(2)}, u32[]{:S(2)}) async-start(bf16[32,2,1024]{2,0,1:T(8,128)(2,1)} %all_to_all.96), calls=%async_computation.2 | async-start | bytes 262144 | tf_op jit(solution)/shard_map/all_to_all | solution.py:170
  52.3 8.1 %copy-start.5 = (s32[16]{0:T(128)S(1)}, s32[16]{0:T(128)}, u32[]{:S(2)}) copy-start(s32[16]{0:T(128)} %param.13) | copy-start | bytes 196
  56.8 15.1 %all-to-all-start = ((bf16[32,2,8192]{2,0,1:T(8,128)(2,1)}), bf16[32,2,8192]{2,0,1:T(8,128)(2,1)S(1)}, u32[]{:S(2)}, u32[]{:S(2)}) async-start(bf16[32,2,8192]{2,0,1:T(8,128)(2,1)} %bitcast.42), calls=%async_computation | async-start | bytes 2097152 | tf_op jit(solution)/shard_map/all_to_all | solution.py:162
  71.9 9.4 %all-to-all-start.3 = ((bf16[64,4,256]{2,0,1:T(8,128)(2,1)}), bf16[64,4,256]{2,0,1:T(8,128)(2,1)S(1)}, u32[]{:S(2)}, u32[]{:S(2)}) async-start(bf16[64,4,256]{2,0,1:T(8,128)(2,1)} %copy.69), calls=%async_computation.3 | async-start | bytes 262144 | tf_op jit(solution)/shard_map/all_to_all | solution.py:188
  81.3 26.6 %all-to-all-start.1 = ((bf16[16,16,2048]{2,1,0:T(8,128)(2,1)}), bf16[16,16,2048]{2,1,0:T(8,128)(2,1)S(1)}, u32[]{:S(2)}, u32[]{:S(2)}) async-start(bf16[16,16,2048]{2,1,0:T(8,128)(2,1)} %bitcast.4), calls=%async_computation.1 | async-start | bytes 2097152 | tf_op jit(solution)/shard_map/all_to_all | solution.py:183
  107.9 1.0 copy-start.1
Sparse Core Ops, SparseCore 0:
  29.6 21.6 all-gather.2
  52.9 22.5 all-gather.4
